TPU v7x, 32 devices: a whole 2x2x4 slice. The times are simulated.
32 devices in a mesh: dp: 16 (over z, y, x), tensor: 2 (over core).
Axes of the slice: x: 2, y: 2, z: 4, core: 2. Of those that a mesh axis runs over, the one named last changes fastest.
Arguments:
- inputs: bfloat16 [4, 8192, 768], P(None, ('dp', 'tensor')), may hold values from -6 to 6
- lengths: int32 [4, 16], P(None, 'dp'), may hold values from 128 to 512, as said below
- bounds: int32 [4, 16], P(None, 'dp'), may hold values from 32 to 384, as said below
- query_matrix: bfloat16 [768, 768], P('dp', 'tensor'), may hold values from -0.21875 to 0.21875
- key_matrix: bfloat16 [768, 768], P('dp', 'tensor'), may hold values from -0.21875 to 0.21875
- value_matrix: bfloat16 [768, 768], P('dp', 'tensor'), may hold values from -0.21875 to 0.21875
- query_value_bias: float32 [2, 768], P(None, 'tensor'), may hold values from -3 to 3
- adapter_down_weight: bfloat16 [2, 768, 8], P(None, 'dp'), may hold values from -0.21875 to 0.21875
- adapter_up_weight: bfloat16 [2, 8, 768], P(None, None, 'tensor'), may hold values from -1 to 1
- attention_output_weight: bfloat16 [768, 768], P('tensor', 'dp'), may hold values from -1.75 to 1.75
- feedforward_input_weight: bfloat16 [768, 3072], P('dp', 'tensor'), may hold values from -0.21875 to 0.21875
- feedforward_input_bias: float32 [3072], P('tensor'), may hold values from -3 to 3
- feedforward_output_weight: bfloat16 [3072, 768], P('tensor', 'dp'), may hold values from -0.109375 to 0.109375
- output_bias: float32 [2, 768], replicated, may hold values from -3 to 3
- layernorm_scale: float32 [2, 768], replicated, may hold values from 0.5 to 1.5
- layernorm_bias: float32 [2, 768], replicated, may hold values from -2 to 2
- output_gradient: bfloat16 [4, 8192, 768], P(None, ('dp', 'tensor')), may hold values from -6 to 6
Outputs:
- outputs: bfloat16 [4, 8192, 768], P(None, ('dp', 'tensor'))
- input_grad: float32 [4, 8192, 768], P(None, ('dp', 'tensor'))
- lora_up_grad: float32 [2, 8, 768], P(None, None, 'tensor')
Inputs may be any that keep to these rules, and one draw needn't show every extreme that they name: Item i of micro-batch m has live positions 0 to lengths[m, i] - 1 of its 512; the others are padding. An item's first segment is positions 0 to bounds - 1, its second bounds to 511; bounds lies between lengths // 4 and 3 * lengths // 4.
All inputs are finite; a program needn't handle non-finite values.
Results may differ from a plain program's by a relative error of at most 0.015.
The roundings to bfloat16 on the way count: a program that leaves them out, or rounds other values in their place, can miss the bound.
Values may be sent and summed in bfloat16 or wider, within the bound.
No kernel may reach another device: no remote copies, remote signals or barrier semaphores. Data moves between devices by JAX's collectives and lax.ppermute only.
A program may use at most 192 MiB of HBM per device.

v0:
```python
import jax
import jax.numpy as jnp
from jax import lax
from jax.sharding import PartitionSpec as P

HEAD_DIM = 64
UPDATE_RANK = 8
SLOT = 512
adapter_scale = 2.0
masked_value = -1000000000.0
norm_eps = 1e-05
highest_precision = lax.Precision.HIGHEST


def layer_norm(value_rows, gain, shift):
    centre = value_rows - jnp.mean(value_rows, axis=-1, keepdims=True)
    spread = jnp.mean(centre * centre, axis=-1, keepdims=True)
    return centre * lax.rsqrt(spread + norm_eps) * gain + shift


def exact_gelu(value_rows):
    return jax.nn.gelu(value_rows, approximate=False)


def item_mask(length, bound):
    places = jnp.arange(SLOT)
    segment = places >= bound
    return (places < length)[None, :] & (segment[:, None] == segment[None, :])


def split_heads(input_array):
    return input_array.reshape(input_array.shape[0], input_array.shape[1] // HEAD_DIM, HEAD_DIM)


def item_scores(query_heads, key_heads, length, bound):
    scores = (
        jnp.einsum("qhd,khd->hqk", query_heads, key_heads, preferred_element_type=jnp.float32)
        * 0.125
    )
    return jnp.where(item_mask(length, bound)[None], scores, masked_value)


def attend_forward(pieces):
    query_rows, keys, value_rows, length, bound = pieces
    query_heads = split_heads(query_rows)
    value_heads = split_heads(value_rows)
    scores = item_scores(query_heads, split_heads(keys), length, bound)
    peak = jnp.max(scores, axis=-1, keepdims=True)
    totals = jnp.log(jnp.sum(jnp.exp(scores - peak), axis=-1, keepdims=True)) + peak
    soft_weights = jnp.exp(scores - totals).astype(jnp.bfloat16)
    mixed = jnp.einsum(
        "hqk,khd->qhd", soft_weights, value_heads, preferred_element_type=jnp.float32
    )
    return (mixed.reshape(SLOT, query_rows.shape[1]).astype(jnp.bfloat16), totals)


def attend_backward(pieces):
    query_rows, keys, value_rows, grad_mixed, totals, length, bound = pieces
    query_heads = split_heads(query_rows)
    key_heads = split_heads(keys)
    grad_heads = split_heads(grad_mixed)
    scores = item_scores(query_heads, key_heads, length, bound)
    probs = jnp.exp(scores - totals)
    value_gradient = jnp.einsum(
        "hqk,qhd->khd", probs.astype(jnp.bfloat16), grad_heads, preferred_element_type=jnp.float32
    )
    grad_probs = jnp.einsum(
        "qhd,khd->hqk", grad_heads, split_heads(value_rows), preferred_element_type=jnp.float32
    )
    inner = jnp.sum(probs * grad_probs, axis=-1, keepdims=True)
    grad_scores = (probs * (grad_probs - inner)).astype(jnp.bfloat16)
    query_gradient = (
        jnp.einsum("hqk,khd->qhd", grad_scores, key_heads, preferred_element_type=jnp.float32)
        * 0.125
    )
    key_gradient = (
        jnp.einsum("hqk,qhd->khd", grad_scores, query_heads, preferred_element_type=jnp.float32)
        * 0.125
    )
    width = query_rows.shape[1]
    return (
        query_gradient.reshape(SLOT, width).astype(jnp.bfloat16),
        key_gradient.reshape(SLOT, width).astype(jnp.bfloat16),
        value_gradient.reshape(SLOT, width).astype(jnp.bfloat16),
    )


def contract_trailing(left, right):
    return lax.dot_general(
        left, right, (((1,), (1,)), ((), ())), preferred_element_type=jnp.float32
    )


def project_row_batch(
    input_rows,
    query_projected,
    key_projected,
    value_projected,
    down_projected,
    query_value_bias,
    adapter_up_weight,
):
    up_weight_float = adapter_up_weight.astype(jnp.float32)
    lowrank_update = jnp.einsum(
        "td,zdr->ztr", input_rows, down_projected, preferred_element_type=jnp.float32
    )
    query_rows = (
        jnp.dot(input_rows, query_projected, preferred_element_type=jnp.float32)
        + query_value_bias[0]
        + adapter_scale
        * jnp.dot(lowrank_update[0], up_weight_float[0], precision=highest_precision)
    ).astype(jnp.bfloat16)
    keys = jnp.dot(input_rows, key_projected, preferred_element_type=jnp.float32).astype(
        jnp.bfloat16
    )
    value_rows = (
        jnp.dot(input_rows, value_projected, preferred_element_type=jnp.float32)
        + query_value_bias[1]
        + adapter_scale
        * jnp.dot(lowrank_update[1], up_weight_float[1], precision=highest_precision)
    ).astype(jnp.bfloat16)
    return (lowrank_update, query_rows, keys, value_rows)


def adapter_components(lowrank_update, query_gradient, value_gradient):
    first_dims = (((0,), (0,)), ((), ()))
    return adapter_scale * jnp.stack(
        [
            lax.dot_general(
                lowrank_update[0],
                query_gradient.astype(jnp.float32),
                first_dims,
                precision=highest_precision,
            ),
            lax.dot_general(
                lowrank_update[1],
                value_gradient.astype(jnp.float32),
                first_dims,
                precision=highest_precision,
            ),
        ]
    )


def input_terms_all(
    query_gradient,
    key_gradient,
    value_gradient,
    query_projected,
    key_projected,
    value_projected,
    down_projected,
    adapter_up_weight,
):
    query_lowrank_gradient = adapter_scale * contract_trailing(query_gradient, adapter_up_weight[0])
    value_lowrank_gradient = adapter_scale * contract_trailing(value_gradient, adapter_up_weight[1])
    down_float = down_projected.astype(jnp.float32)
    total = contract_trailing(query_gradient, query_projected)
    total = total + contract_trailing(key_gradient, key_projected)
    total = total + contract_trailing(value_gradient, value_projected)
    total = total + lax.dot_general(
        query_lowrank_gradient, down_float[0], (((1,), (1,)), ((), ())), precision=highest_precision
    )
    total = total + lax.dot_general(
        value_lowrank_gradient, down_float[1], (((1,), (1,)), ((), ())), precision=highest_precision
    )
    return total


def forward_pass(rows_local, item_lengths, item_bounds, gathered, parameters):
    (
        query_projected,
        key_projected,
        value_projected,
        down_projected,
        out_full,
        ffn_in_full,
        ffn_out_full,
    ) = gathered
    (
        query_value_bias,
        adapter_up_weight,
        feedforward_input_bias,
        output_bias,
        layernorm_scale,
        layernorm_bias,
    ) = parameters
    group_items = item_lengths.shape[0]
    row_groups = lax.all_gather(rows_local, "tensor", axis=0, tiled=True)
    lowrank_update, query_rows, keys, value_rows = project_row_batch(
        row_groups,
        query_projected,
        key_projected,
        value_projected,
        down_projected,
        query_value_bias,
        adapter_up_weight,
    )
    width = query_rows.shape[1]
    item_shape = (group_items, SLOT, width)
    mixed, totals = lax.map(
        attend_forward,
        (
            query_rows.reshape(item_shape),
            keys.reshape(item_shape),
            value_rows.reshape(item_shape),
            item_lengths,
            item_bounds,
        ),
    )
    mixed_rows = mixed.reshape(group_items * SLOT, width)
    attended = lax.psum_scatter(
        jnp.dot(mixed_rows, out_full, preferred_element_type=jnp.float32),
        "tensor",
        scatter_dimension=0,
        tiled=True,
    )
    hidden_sum = rows_local.astype(jnp.float32) + attended + output_bias[0]
    normed = layer_norm(hidden_sum, layernorm_scale[0], layernorm_bias[0])
    pre_act = (
        jnp.dot(
            lax.all_gather(normed.astype(jnp.bfloat16), "tensor", axis=0, tiled=True),
            ffn_in_full,
            preferred_element_type=jnp.float32,
        )
        + feedforward_input_bias
    )
    activated = exact_gelu(pre_act).astype(jnp.bfloat16)
    ffn_total = (
        normed
        + lax.psum_scatter(
            jnp.dot(activated, ffn_out_full, preferred_element_type=jnp.float32),
            "tensor",
            scatter_dimension=0,
            tiled=True,
        )
        + output_bias[1]
    )
    result = layer_norm(ffn_total, layernorm_scale[1], layernorm_bias[1]).astype(jnp.bfloat16)
    kept = (lowrank_update, query_rows, keys, value_rows, totals, hidden_sum, pre_act, ffn_total)
    return (result, kept)


def layer_backward(grad_out, item_lengths, item_bounds, gathered, parameters, kept):
    (
        query_projected,
        key_projected,
        value_projected,
        down_projected,
        out_full,
        ffn_in_full,
        ffn_out_full,
    ) = gathered
    (
        query_value_bias,
        adapter_up_weight,
        feedforward_input_bias,
        output_bias,
        layernorm_scale,
        layernorm_bias,
    ) = parameters
    lowrank_update, query_rows, keys, value_rows, totals, hidden_sum, pre_act, ffn_total = kept
    group_items = item_lengths.shape[0]
    outer_pull = jax.vjp(
        lambda field: layer_norm(field, layernorm_scale[1], layernorm_bias[1]), ffn_total
    )[1]
    grad_sum = outer_pull(grad_out.astype(jnp.float32))[0]
    grad_act = contract_trailing(
        lax.all_gather(grad_sum.astype(jnp.bfloat16), "tensor", axis=0, tiled=True), ffn_out_full
    )
    gelu_pull = jax.vjp(exact_gelu, pre_act)[1]
    grad_pre = gelu_pull(grad_act)[0].astype(jnp.bfloat16)
    grad_normed = grad_sum + lax.psum_scatter(
        contract_trailing(grad_pre, ffn_in_full), "tensor", scatter_dimension=0, tiled=True
    )
    inner_pull = jax.vjp(
        lambda field: layer_norm(field, layernorm_scale[0], layernorm_bias[0]), hidden_sum
    )[1]
    grad_hidden = inner_pull(grad_normed)[0]
    grad_mixed = contract_trailing(
        lax.all_gather(grad_hidden.astype(jnp.bfloat16), "tensor", axis=0, tiled=True), out_full
    ).astype(jnp.bfloat16)
    width = query_rows.shape[1]
    item_shape = (group_items, SLOT, width)
    query_gradient, key_gradient, value_gradient = lax.map(
        attend_backward,
        (
            query_rows.reshape(item_shape),
            keys.reshape(item_shape),
            value_rows.reshape(item_shape),
            grad_mixed.reshape(item_shape),
            totals,
            item_lengths,
            item_bounds,
        ),
    )
    query_gradient = query_gradient.reshape(group_items * SLOT, width)
    key_gradient = key_gradient.reshape(group_items * SLOT, width)
    value_gradient = value_gradient.reshape(group_items * SLOT, width)
    adapter_portion = adapter_components(lowrank_update, query_gradient, value_gradient)
    row_gradient = grad_hidden + lax.psum_scatter(
        input_terms_all(
            query_gradient,
            key_gradient,
            value_gradient,
            query_projected,
            key_projected,
            value_projected,
            down_projected,
            adapter_up_weight,
        ).astype(jnp.bfloat16),
        "tensor",
        scatter_dimension=0,
        tiled=True,
    ).astype(jnp.float32)
    return (row_gradient, adapter_portion)


def local(
    inputs,
    lengths,
    bounds,
    query_matrix,
    key_matrix,
    value_matrix,
    query_value_bias,
    adapter_down_weight,
    adapter_up_weight,
    attention_output_weight,
    feedforward_input_weight,
    feedforward_input_bias,
    feedforward_output_weight,
    output_bias,
    layernorm_scale,
    layernorm_bias,
    output_gradient,
):
    micro_count = inputs.shape[0]
    parameters = (
        query_value_bias,
        adapter_up_weight,
        feedforward_input_bias,
        output_bias,
        layernorm_scale,
        layernorm_bias,
    )
    result_list = []
    gradient_tree = []
    adapter_combined = jnp.zeros((2, UPDATE_RANK, adapter_up_weight.shape[2]), jnp.float32)
    for batch_index in range(micro_count):
        forward_set = (
            lax.all_gather(query_matrix, "dp", axis=0, tiled=True),
            lax.all_gather(key_matrix, "dp", axis=0, tiled=True),
            lax.all_gather(value_matrix, "dp", axis=0, tiled=True),
            lax.all_gather(adapter_down_weight, "dp", axis=1, tiled=True),
            lax.all_gather(attention_output_weight, "dp", axis=1, tiled=True),
            lax.all_gather(feedforward_input_weight, "dp", axis=0, tiled=True),
            lax.all_gather(feedforward_output_weight, "dp", axis=1, tiled=True),
        )
        result, kept = forward_pass(
            inputs[batch_index], lengths[batch_index], bounds[batch_index], forward_set, parameters
        )
        backward_set = (
            lax.all_gather(query_matrix, "dp", axis=0, tiled=True),
            lax.all_gather(key_matrix, "dp", axis=0, tiled=True),
            lax.all_gather(value_matrix, "dp", axis=0, tiled=True),
            lax.all_gather(adapter_down_weight, "dp", axis=1, tiled=True),
            lax.all_gather(attention_output_weight, "dp", axis=1, tiled=True),
            lax.all_gather(feedforward_input_weight, "dp", axis=0, tiled=True),
            lax.all_gather(feedforward_output_weight, "dp", axis=1, tiled=True),
        )
        row_gradient, adapter_portion = layer_backward(
            output_gradient[batch_index],
            lengths[batch_index],
            bounds[batch_index],
            backward_set,
            parameters,
            kept,
        )
        adapter_combined = adapter_combined + lax.psum(adapter_portion, "dp")
        result_list.append(result)
        gradient_tree.append(row_gradient)
    return (jnp.stack(result_list), jnp.stack(gradient_tree), adapter_combined)


def solution(mesh):
    return jax.shard_map(
        local,
        mesh=mesh,
        in_specs=(
            P(None, ("dp", "tensor"), None),
            P(None, "dp"),
            P(None, "dp"),
            P("dp", "tensor"),
            P("dp", "tensor"),
            P("dp", "tensor"),
            P(None, "tensor"),
            P(None, "dp", None),
            P(None, None, "tensor"),
            P("tensor", "dp"),
            P("dp", "tensor"),
            P("tensor"),
            P("tensor", "dp"),
            P(),
            P(),
            P(),
            P(None, ("dp", "tensor"), None),
        ),
        out_specs=(
            P(None, ("dp", "tensor"), None),
            P(None, ("dp", "tensor"), None),
            P(None, None, "tensor"),
        ),
        check_vma=False,
    )
```

profile of v0, /device:TPU:0, one launch (start us, length us, event | category | flops | bytes accessed | tf_op | source)
XLA Modules:
  0.0 771.6 jit_solution(13941130316083166364)
XLA Ops:
  12.5 44.5 %all_gather.48 = bf16[2,768,8]{2,0,1:T(2,128)(2,1)S(1)} all-gather(bf16[2,48,8]{2,0,1:T(2,128)(2,1)S(1)} %copy.57), channel_id=1, replica_groups=mesh['dp'=16,'tensor'=2] {'dp'}, dimensions={1}, use_global_device_ids=true | all-gather | bytes 26112 | tf_op jit(solution)/shard_map/all_gather | solution.py:355
  57.3 39.2 %all_gather.49 = bf16[768,384]{1,0:T(8,128)(2,1)S(1)} all-gather(bf16[48,384]{1,0:T(8,128)(2,1)} %param.20), channel_id=1, replica_groups=mesh['dp'=16,'tensor'=2] {'dp'}, dimensions={0}, use_global_device_ids=true | all-gather | bytes 626688 | tf_op jit(solution)/shard_map/all_gather | solution.py:352
  96.5 41.1 %all_gather.50 = bf16[768,384]{1,0:T(8,128)(2,1)S(1)} all-gather(bf16[48,384]{1,0:T(8,128)(2,1)} %param.21), channel_id=1, replica_groups=mesh['dp'=16,'tensor'=2] {'dp'}, dimensions={0}, use_global_device_ids=true | all-gather | bytes 626688 | tf_op jit(solution)/shard_map/all_gather | solution.py:353
  137.5 39.3 %all_gather.47 = bf16[768,384]{1,0:T(8,128)(2,1)S(1)} all-gather(bf16[48,384]{1,0:T(8,128)(2,1)} %param.22), channel_id=1, replica_groups=mesh['dp'=16,'tensor'=2] {'dp'}, dimensions={0}, use_global_device_ids=true | all-gather | bytes 626688 | tf_op jit(solution)/shard_map/all_gather | solution.py:354
  176.8 40.8 %all_gather.51 = bf16[384,768]{0,1:T(8,128)(2,1)S(1)} all-gather(bf16[384,48]{0,1:T(8,128)(2,1)} %param.26), channel_id=1, replica_groups=mesh['dp'=16,'tensor'=2] {'dp'}, dimensions={1}, use_global_device_ids=true | all-gather | bytes 626688 | tf_op jit(solution)/shard_map/all_gather | solution.py:356
  280.6 4.3 fusion.188
  289.5 47.2 %all-gather.7.cloned.1.call-done = bf16[768,1536]{1,0:T(8,128)(2,1)} async-done(((bf16[48,1536]{1,0:T(8,128)(2,1)}), bf16[768,1536]{1,0:T(8,128)(2,1)}) %all-gather.7.cloned.1.call-update) | async-done | bytes 2359312 | tf_op jit(solution)/shard_map/all_gather | solution.py:357
  336.7 10.4 %fusion.11 = (f32[512,1536]{1,0:T(8,128)}, f32[512,1536]{1,0:T(8,128)}) fusion(f32[1536]{0:T(1024)S(1)} %copy-done.198, bf16[512,768]{1,0:T(8,128)(2,1)S(1)} %all_gather.60, bf16[768,1536]{1,0:T(8,128)(2,1)} %all-gather.7.cloned.1.call-done), kind=kOutput, calls=%fused_computation.39 | convolution fusion | flops 1257504768 | bytes 9443328 | tf_op jit(solution)/shard_map/dot_general | solution.py:221
  347.2 52.7 %all-gather.9.cloned.1.call-done = bf16[1536,768]{0,1:T(8,128)(2,1)} async-done(((bf16[1536,48]{0,1:T(8,128)(2,1)}), bf16[1536,768]{0,1:T(8,128)(2,1)}) %all-gather.9.cloned.1.call-update) | async-done | bytes 2359312 | tf_op jit(solution)/shard_map/all_gather | solution.py:358
  399.9 6.1 fusion.35
  408.4 9.7 %fusion.10 = (f32[512,1536]{1,0:T(8,128)S(1)}, f32[512,1536]{1,0:T(8,128)S(1)}) fusion(f32[1536]{0:T(1024)} %param.28, bf16[512,768]{1,0:T(8,128)(2,1)S(1)} %all_gather.58, bf16[768,1536]{1,0:T(8,128)(2,1)} %all-gather.7.cloned.1.call-done), kind=kOutput, calls=%fused_computation.38 | convolution fusion | flops 1257504768 | bytes 9443328 | tf_op jit(solution)/shard_map/dot_general | solution.py:221
  425.9 9.5 %fusion.9 = (f32[512,1536]{1,0:T(8,128)S(1)}, f32[512,1536]{1,0:T(8,128)S(1)}) fusion(f32[1536]{0:T(1024)} %param.28, bf16[512,768]{1,0:T(8,128)(2,1)S(1)} %all_gather.56, bf16[768,1536]{1,0:T(8,128)(2,1)} %all-gather.7.cloned.1.call-done), kind=kOutput, calls=%fused_computation.37 | convolution fusion | flops 1257504768 | bytes 9443328 | tf_op jit(solution)/shard_map/dot_general | solution.py:221
  442.4 5.9 reduce-scatter.23.cloned.1.call-done
  448.4 4.5 fusion.187
  455.2 8.1 %fusion.8 = (f32[512,1536]{1,0:T(8,128)S(1)}, f32[512,1536]{1,0:T(8,128)S(1)}) fusion(f32[1536]{0:T(1024)S(1)} %copy-done.199, bf16[512,768]{1,0:T(8,128)(2,1)S(1)} %all_gather.52, bf16[768,1536]{1,0:T(8,128)(2,1)S(1)} %copy-done.197), kind=kOutput, calls=%fused_computation.36 | convolution fusion | flops 1257504768 | bytes 9443328 | tf_op jit(solution)/shard_map/dot_general | solution.py:221
  468.7 10.4 %reduce-scatter.19.cloned.1.call-done = f32[256,768]{1,0:T(8,128)} async-done(((f32[512,768]{1,0:T(8,128)}), f32[256,768]{1,0:T(8,128)}) %reduce-scatter.19.cloned.1.call-update) | async-done | bytes 786448 | tf_op jit(solution)/shard_map/reduce_scatter | solution.py:231
  489.2 7.8 %fusion.43 = f32[512,768]{1,0:T(8,128)} fusion(bf16[768,1536]{1,0:T(8,128)(2,1)} %all-gather.7.cloned.1.call-done, f32[512,1536]{1,0:T(8,128)} %get-tuple-element.339, f32[512,1536]{1,0:T(8,128)} %get-tuple-element.340, bf16[512,768]{1,0:T(8,128)(2,1)} %all_gather.67, bf16[1536,768]{0,1:T(8,128)(2,1)S(1)} %copy-done.4), kind=kOutput, calls=%fused_computation.117 | convolution fusion | flops 2426929152 | bytes 13369344 | tf_op jit(solution)/shard_map/dot_general | solution.py:89
  499.1 4.4 fusion.181
  507.1 7.8 %fusion.42 = f32[512,768]{1,0:T(8,128)} fusion(bf16[768,1536]{1,0:T(8,128)(2,1)} %all-gather.7.cloned.1.call-done, f32[512,1536]{1,0:T(8,128)} %copy-done.82, f32[512,1536]{1,0:T(8,128)} %copy-done.83, bf16[512,768]{1,0:T(8,128)(2,1)} %all_gather.65, bf16[1536,768]{0,1:T(8,128)(2,1)S(1)} %copy-done.4), kind=kOutput, calls=%fused_computation.116 | convolution fusion | flops 2426929152 | bytes 13369344 | tf_op jit(solution)/shard_map/dot_general | solution.py:89
  519.1 8.3 %fusion.40 = f32[512,768]{1,0:T(8,128)} fusion(bf16[768,1536]{1,0:T(8,128)(2,1)} %all-gather.7.cloned.1.call-done, f32[512,1536]{1,0:T(8,128)} %copy-done.84, f32[512,1536]{1,0:T(8,128)} %copy-done.85, bf16[512,768]{1,0:T(8,128)(2,1)} %all_gather.61, bf16[1536,768]{0,1:T(8,128)(2,1)S(1)} %copy-done.4), kind=kOutput, calls=%fused_computation.114 | convolution fusion | flops 2426929152 | bytes 13369344 | tf_op jit(solution)/shard_map/dot_general | solution.py:89
  531.3 7.8 %fusion.41 = f32[512,768]{1,0:T(8,128)} fusion(bf16[768,1536]{1,0:T(8,128)(2,1)} %all-gather.7.cloned.1.call-done, f32[512,1536]{1,0:T(8,128)} %copy-done.80, f32[512,1536]{1,0:T(8,128)} %copy-done.81, bf16[512,768]{1,0:T(8,128)(2,1)} %all_gather.63, bf16[1536,768]{0,1:T(8,128)(2,1)S(1)} %copy-done.4), kind=kOutput, calls=%fused_computation.115 | convolution fusion | flops 2426929152 | bytes 13369344 | tf_op jit(solution)/shard_map/dot_general | solution.py:89
  545.2 5.8 reduce-scatter.37.cloned.1.call-done
  556.9 4.6 convolution_convert_fusion.6
  588.9 4.6 multiply_reduce_fusion.3
  593.6 6.5 multiply_convert_fusion.3
  603.3 4.8 multiply_reduce_fusion.2
  608.2 4.7 multiply_reduce_fusion.1
  612.8 5.6 multiply_reduce_fusion
  622.1 6.7 multiply_convert_fusion.2
  630.5 4.9 multiply_convert_fusion.1
  637.3 4.7 multiply_convert_fusion
  676.5 77.1 %psum.34 = f32[2,8,384]{2,1,0:T(8,128)} all-reduce(f32[2,8,384]{2,1,0:T(8,128)S(1)} %fusion.110), channel_id=1, replica_groups=mesh['dp'=16,'tensor'=2] {'dp'}, use_global_device_ids=true, to_apply=%region_60.61 | all-reduce | flops 6144 | bytes 49152 | tf_op jit(solution)/shard_map/psum | solution.py:380
  (670 shorter events, 213.0 us)
Async XLA Ops:
  8.0 270.0 %reduce-scatter.21.cloned.1.call-start = ((), (), s32[]{:S(2)}) async-start(), calls=%async_computation.20 | async-start | bytes 2359296 | tf_op jit(solution)/shard_map/reduce_scatter | solution.py:212
  57.3 207.3 %copy-start.88 = (bf16[2,768,8]{1,2,0:T(8,128)(2,1)}, bf16[2,768,8]{1,2,0:T(8,128)(2,1)S(1)}, u32[]{:S(2)}) copy-start(bf16[2,768,8]{1,2,0:T(8,128)(2,1)S(1)} %copy.58) | copy-start | bytes 73732
  57.3 160.3 %copy-start.53 = (bf16[4,256,768]{2,1,0:T(8,128)(2,1)S(1)}, bf16[4,256,768]{2,1,0:T(8,128)(2,1)}, u32[]{:S(2)}) copy-start(bf16[4,256,768]{2,1,0:T(8,128)(2,1)} %param.17) | copy-start | bytes 4718596
  96.5 168.4 %copy-start.19 = (bf16[768,384]{1,0:T(8,128)(2,1)}, bf16[768,384]{1,0:T(8,128)(2,1)S(1)}, u32[]{:S(2)}) copy-start(bf16[768,384]{1,0:T(8,128)(2,1)S(1)} %all_gather.49) | copy-start | bytes 1769476
  137.5 129.9 %copy-start.14 = (bf16[768,384]{1,0:T(8,128)(2,1)}, bf16[768,384]{1,0:T(8,128)(2,1)S(1)}, u32[]{:S(2)}) copy-start(bf16[768,384]{1,0:T(8,128)(2,1)S(1)} %all_gather.50) | copy-start | bytes 1769476
  176.8 93.8 %copy-start.22 = (bf16[768,384]{1,0:T(8,128)(2,1)}, bf16[768,384]{1,0:T(8,128)(2,1)S(1)}, u32[]{:S(2)}) copy-start(bf16[768,384]{1,0:T(8,128)(2,1)S(1)} %all_gather.47) | copy-start | bytes 1769476
  217.6 56.1 %copy-start.24 = (bf16[384,768]{0,1:T(8,128)(2,1)}, bf16[384,768]{0,1:T(8,128)(2,1)S(1)}, u32[]{:S(2)}) copy-start(bf16[384,768]{0,1:T(8,128)(2,1)S(1)} %all_gather.51) | copy-start | bytes 1769476
  232.9 45.1 %reduce-scatter.17.cloned.1.call-start = ((), (), s32[]{:S(2)}) async-start(), calls=%async_computation.16 | async-start | bytes 2359296 | tf_op jit(solution)/shard_map/reduce_scatter | solution.py:212
  247.3 30.7 %reduce-scatter.29.cloned.1.call-start = ((), (), s32[]{:S(2)}) async-start(), calls=%async_computation.24 | async-start | bytes 2359296 | tf_op jit(solution)/shard_map/reduce_scatter | solution.py:212
  261.3 19.3 %reduce-scatter.25.cloned.1.call-start = ((), (), s32[]{:S(2)}) async-start(), calls=%async_computation.22 | async-start | bytes 2359296 | tf_op jit(solution)/shard_map/reduce_scatter | solution.py:212
  275.5 61.2 %all-gather.7.cloned.1.call-start = ((), (), s32[]{:S(2)}) async-start(), calls=%async_computation.17 | async-start | bytes 2506752 | tf_op jit(solution)/shard_map/all_gather | solution.py:357
  276.1 123.8 %all-gather.9.cloned.1.call-start = ((), (), s32[]{:S(2)}) async-start(), calls=%async_computation.18 | async-start | bytes 2506752 | tf_op jit(solution)/shard_map/all_gather | solution.py:358
  276.7 165.7 %reduce-scatter.31.cloned.1.call-start = ((), (), s32[]{:S(2)}) async-start(), calls=%async_computation.25 | async-start | bytes 2359296 | tf_op jit(solution)/shard_map/reduce_scatter | solution.py:231
  285.1 51.6 %copy-start.198 = (f32[1536]{0:T(1024)S(1)}, f32[1536]{0:T(1024)}, u32[]{:S(2)}) copy-start(f32[1536]{0:T(1024)} %param.28) | copy-start | bytes 18436
  406.0 36.4 %reduce-scatter.27.cloned.1.call-start = ((), (), s32[]{:S(2)}) async-start(), calls=%async_computation.23 | async-start | bytes 2359296 | tf_op jit(solution)/shard_map/reduce_scatter | solution.py:231
  423.4 24.9 %reduce-scatter.23.cloned.1.call-start = ((), (), s32[]{:S(2)}) async-start(), calls=%async_computation.21 | async-start | bytes 2359296 | tf_op jit(solution)/shard_map/reduce_scatter | solution.py:231
  440.7 38.3 %reduce-scatter.19.cloned.1.call-start = ((), (), s32[]{:S(2)}) async-start(), calls=%async_computation.19 | async-start | bytes 2359296 | tf_op jit(solution)/shard_map/reduce_scatter | solution.py:231
  442.4 36.7 %copy-start.154 = (f32[256]{0:T(256)}, f32[256]{0:T(256)S(1)}, u32[]{:S(2)}) copy-start(f32[256]{0:T(256)S(1)} %fusion.147) | copy-start | bytes 3076
  468.6 73.4 %reduce-scatter.45.cloned.1.call-start = ((), (), s32[]{:S(2)}) async-start(), calls=%async_computation.32 | async-start | bytes 2359296 | tf_op jit(solution)/shard_map/reduce_scatter | solution.py:273
  497.0 45.0 %reduce-scatter.41.cloned.1.call-start = ((), (), s32[]{:S(2)}) async-start(), calls=%async_computation.30 | async-start | bytes 2359296 | tf_op jit(solution)/shard_map/reduce_scatter | solution.py:273
  514.9 27.1 %reduce-scatter.33.cloned.1.call-start = ((), (), s32[]{:S(2)}) async-start(), calls=%async_computation.26 | async-start | bytes 2359296 | tf_op jit(solution)/shard_map/reduce_scatter | solution.py:273
  527.5 23.6 %reduce-scatter.37.cloned.1.call-start = ((), (), s32[]{:S(2)}) async-start(), calls=%async_computation.28 | async-start | bytes 2359296 | tf_op jit(solution)/shard_map/reduce_scatter | solution.py:273
  539.1 214.4 %reduce-scatter.35.cloned.1.call-start = ((), (), s32[]{:S(2)}) async-start(), calls=%async_computation.27 | async-start | bytes 1179648 | tf_op jit(solution)/shard_map/reduce_scatter | solution.py:301
  622.1 133.6 %reduce-scatter.39.cloned.1.call-start = ((), (), s32[]{:S(2)}) async-start(), calls=%async_computation.29 | async-start | bytes 1179648 | tf_op jit(solution)/shard_map/reduce_scatter | solution.py:301
  649.9 107.8 %reduce-scatter.43.cloned.1.call-start = ((), (), s32[]{:S(2)}) async-start(), calls=%async_computation.31 | async-start | bytes 1179648 | tf_op jit(solution)/shard_map/reduce_scatter | solution.py:301
  659.8 100.1 %reduce-scatter.47.cloned.1.call-start = ((), (), s32[]{:S(2)}) async-start(), calls=%async_computation.33 | async-start | bytes 1179648 | tf_op jit(solution)/shard_map/reduce_scatter | solution.py:301
  667.1 86.5 %copy-start.174 = (f32[256]{0:T(256)S(1)}, f32[256]{0:T(256)}, u32[]{:S(2)}) copy-start(f32[256]{0:T(256)} %copy-done.173) | copy-start | bytes 3076
  669.2 84.4 %copy-start.33 = (f32[256,768]{1,0:T(8,128)S(1)}, f32[256,768]{1,0:T(8,128)}, u32[]{:S(2)}) copy-start(f32[256,768]{1,0:T(8,128)} %copy-done.32) | copy-start | bytes 2359300
  669.2 86.4 %copy-start.37 = (f32[256,768]{1,0:T(8,128)S(1)}, f32[256,768]{1,0:T(8,128)}, u32[]{:S(2)}) copy-start(f32[256,768]{1,0:T(8,128)} %copy-done.36) | copy-start | bytes 2359300
  669.2 88.5 %copy-start.35 = (f32[256,768]{1,0:T(8,128)S(1)}, f32[256,768]{1,0:T(8,128)}, u32[]{:S(2)}) copy-start(f32[256,768]{1,0:T(8,128)} %copy-done.34) | copy-start | bytes 2359300
  674.2 85.6 %copy-start.40 = (f32[256,768]{1,0:T(8,128)S(1)}, f32[256,768]{1,0:T(8,128)}, u32[]{:S(2)}) copy-start(f32[256,768]{1,0:T(8,128)} %copy-done.39) | copy-start | bytes 2359300
  674.2 85.6 %copy-start.178 = (f32[256]{0:T(256)S(1)}, f32[256]{0:T(256)}, u32[]{:S(2)}) copy-start(f32[256]{0:T(256)} %copy-done.177) | copy-start | bytes 3076
  (200 other events, 889.0 us)
Sparse Core Ops, SparseCore 0:
  233.0 5.0 reduce-scatter.20
  247.4 5.1 reduce-scatter.16
  261.5 5.1 reduce-scatter.28
  275.6 4.9 reduce-scatter.24
  406.1 7.4 reduce-scatter.30
  423.6 7.4 reduce-scatter.26
  440.8 7.4 reduce-scatter.22
  468.7 10.3 reduce-scatter.18
  497.1 10.3 reduce-scatter.44
  515.0 10.3 reduce-scatter.40
  528.2 10.3 reduce-scatter.32
  540.7 10.3 reduce-scatter.36
  622.2 9.4 reduce-scatter.34
  650.1 9.4 reduce-scatter.38
  661.6 9.2 reduce-scatter.42
  673.6 9.2 reduce-scatter.46
Sparse Core Ops, SparseCore 1:
  278.8 57.9 all-gather.6
  339.4 60.4 all-gather.8
where the time goes:
time: 779 us; the launch traced here: 772 us
  blocking collectives  324 us (42%)
  matrix products  197 us (25%)
  waiting for transfers between devices  126 us (16%)
  other arithmetic  82.3 us (11%)
  local copies, waits for them, and re-layouts  22 us (3%)
  between operations  18.9 us (2%)
    psum x1, blocking collectives, local(): adapter_combined = adapter_combined + lax.psum(adapter_portion, 'dp')  77.1 us
    dot_general x28, matrix products, contract_trailing(): lax.dot_general(left, right, (((1,), (1,)), ((), ())), preferred_element_...  53.7 us
    all_gather x1, waiting for transfers between devices, local(): lax.all_gather(feedforward_output_weight, 'dp', axis=1, tiled=True)  52.7 us
    all_gather x1, waiting for transfers between devices, local(): lax.all_gather(feedforward_input_weight, 'dp', axis=0, tiled=True)  47.2 us
    all_gather x1, blocking collectives, local(): lax.all_gather(adapter_down_weight, 'dp', axis=1, tiled=True)  44.5 us
    all_gather x1, blocking collectives, local(): lax.all_gather(key_matrix, 'dp', axis=0, tiled=True)  41.1 us
    all_gather x1, blocking collectives, local(): lax.all_gather(attention_output_weight, 'dp', axis=1, tiled=True)  40.8 us
    all_gather x1, blocking collectives, local(): lax.all_gather(value_matrix, 'dp', axis=0, tiled=True)  39.3 us
  transfers between devices with their start and end apart: 18, of which 6 were waited for; matrix products, arithmetic and copies ran while one was open for 22% of the time, Pallas kernels for 0%

commit v1 on v0

--- a/solution.py
+++ b/solution.py
@@ -1,3 +1,4 @@
+import functools
 import jax
 import jax.numpy as jnp
 from jax import lax
@@ -10,6 +11,30 @@
 masked_value = -1000000000.0
 norm_eps = 1e-05
 highest_precision = lax.Precision.HIGHEST
+
+
+def area_test(obj, dim_i):
+    tall, block_last, w_next = (lax.axis_size("dp"), lax.axis_index("dp"), obj.shape[dim_i])
+    all_rows = tuple((dev_j * tall if i == dim_i else dev_j for i, dev_j in enumerate(obj.shape)))
+    ready = lax.dynamic_update_slice_in_dim(
+        jnp.zeros(all_rows, obj.dtype), obj, block_last * w_next, axis=dim_i
+    )
+    inter = block_now = obj
+    for no in [*range(1, tall // 2 + 1)]:
+        inter = lax.ppermute(inter, "dp", tuple(((i, (i + 1) % tall) for i in range(tall))))
+        ready = lax.dynamic_update_slice_in_dim(
+            ready, inter, (block_last - no) % tall * w_next, axis=dim_i
+        )
+        if 2 * no < tall:
+            latest = tuple(((i, (i - 1) % tall) for i in range(tall)))
+            block_now = lax.ppermute(block_now, "dp", latest)
+            ready = lax.dynamic_update_slice_in_dim(
+                ready, block_now, (block_last + no) % tall * w_next, axis=dim_i
+            )
+    return ready
+
+
+post_pages = functools.partial(area_test, dim_i=1)
 
 
 def layer_norm(value_rows, gain, shift):
@@ -353,7 +378,7 @@
             lax.all_gather(key_matrix, "dp", axis=0, tiled=True),
             lax.all_gather(value_matrix, "dp", axis=0, tiled=True),
             lax.all_gather(adapter_down_weight, "dp", axis=1, tiled=True),
-            lax.all_gather(attention_output_weight, "dp", axis=1, tiled=True),
+            post_pages(attention_output_weight),
             lax.all_gather(feedforward_input_weight, "dp", axis=0, tiled=True),
             lax.all_gather(feedforward_output_weight, "dp", axis=1, tiled=True),
         )

time: 779 us -> 839 us (1.077)
  starting transfers between devices: 1.18 us -> 42.9 us
  matrix products: 197 us -> 210 us
  waiting for transfers between devices: 126 us -> 138 us
    ppermute x0 -> x15, starting transfers between devices: none -> 41.1 us  [the longest x7 36.6 us: area_test(): block_now = lax.ppermute(block_now, 'dp', latest)]
    ppermute x0 -> x15, waiting for transfers between devices: none -> 17.3 us  [the longest x8 17.3 us: area_test(): lax.ppermute(inter, 'dp', tuple(((i, (i + 1) % tall) for i in range(tall))))]
  transfers between devices with their start and end apart: 18 -> 33, of which waited for: 6 -> 12; matrix products, arithmetic and copies ran while one was open for 22% -> 24% of each run, Pallas kernels for 0% -> 0%
where the time goes in v1:
time: 839 us; the launch traced here: 835 us
  blocking collectives  318 us (38%)
  matrix products  210 us (25%)
  waiting for transfers between devices  138 us (16%)
  other arithmetic  82.8 us (10%)
  starting transfers between devices  42.9 us (5%)
  local copies, waits for them, and re-layouts  23.1 us (3%)
  between operations  19.4 us (2%)
    psum x1, blocking collectives, local(): adapter_combined = adapter_combined + lax.psum(adapter_portion, 'dp')  71.8 us
    dot_general x28, matrix products, contract_trailing(): lax.dot_general(left, right, (((1,), (1,)), ((), ())), preferred_element_...  53.6 us
    all_gather x1, waiting for transfers between devices, local(): lax.all_gather(feedforward_output_weight, 'dp', axis=1, tiled=True)  52.7 us
    all_gather x1, blocking collectives, local(): lax.all_gather(attention_output_weight, 'dp', axis=1, tiled=True)  46.8 us
    all_gather x1, waiting for transfers between devices, local(): lax.all_gather(feedforward_input_weight, 'dp', axis=0, tiled=True)  45.4 us
    all_gather x1, blocking collectives, local(): lax.all_gather(query_matrix, 'dp', axis=0, tiled=True)  40.7 us
    all_gather x1, blocking collectives, local(): lax.all_gather(adapter_down_weight, 'dp', axis=1, tiled=True)  39.7 us
    all_gather x1, blocking collectives, local(): lax.all_gather(key_matrix, 'dp', axis=0, tiled=True)  39.4 us
  transfers between devices with their start and end apart: 33, of which 12 were waited for; matrix products, arithmetic and copies ran while one was open for 24% of the time, Pallas kernels for 0%

profile of v1, /device:TPU:0, one launch (start us, length us, event | category | flops | bytes accessed | tf_op | source)
XLA Modules:
  0.0 834.6 jit_solution(10733430360642614149)
XLA Ops:
  15.9 39.7 %all_gather.48 = bf16[2,768,8]{2,0,1:T(2,128)(2,1)S(1)} all-gather(bf16[2,48,8]{2,0,1:T(2,128)(2,1)S(1)} %copy.57), channel_id=1, replica_groups=mesh['dp'=16,'tensor'=2] {'dp'}, dimensions={1}, use_global_device_ids=true | all-gather | bytes 26112 | tf_op jit(solution)/shard_map/all_gather | solution.py:380
  55.9 39.4 %all_gather.50 = bf16[768,384]{1,0:T(8,128)(2,1)S(1)} all-gather(bf16[48,384]{1,0:T(8,128)(2,1)} %param.21), channel_id=1, replica_groups=mesh['dp'=16,'tensor'=2] {'dp'}, dimensions={0}, use_global_device_ids=true | all-gather | bytes 626688 | tf_op jit(solution)/shard_map/all_gather | solution.py:378
  104.4 40.7 %all_gather.49 = bf16[768,384]{1,0:T(8,128)(2,1)S(1)} all-gather(bf16[48,384]{1,0:T(8,128)(2,1)S(1)} %copy-done.158), channel_id=1, replica_groups=mesh['dp'=16,'tensor'=2] {'dp'}, dimensions={0}, use_global_device_ids=true | all-gather | bytes 626688 | tf_op jit(solution)/shard_map/all_gather | solution.py:377
  149.3 39.4 %all_gather.47 = bf16[768,384]{1,0:T(8,128)(2,1)S(1)} all-gather(bf16[48,384]{1,0:T(8,128)(2,1)S(1)} %copy-done.159), channel_id=1, replica_groups=mesh['dp'=16,'tensor'=2] {'dp'}, dimensions={0}, use_global_device_ids=true | all-gather | bytes 626688 | tf_op jit(solution)/shard_map/all_gather | solution.py:379
  199.1 5.4 convolution_convert_fusion.12
  216.6 5.7 collective-permute-start.5
  224.2 5.7 collective-permute-start.7
  231.7 5.7 collective-permute-start.9
  239.3 5.7 collective-permute-start.11
  246.8 5.7 collective-permute-start.13
  254.4 7.5 collective-permute-done.14
  308.9 5.1 reduce-scatter.25.cloned.1.call-done
  322.1 45.4 %all-gather.7.cloned.1.call-done = bf16[768,1536]{1,0:T(8,128)(2,1)} async-done(((bf16[48,1536]{1,0:T(8,128)(2,1)}), bf16[768,1536]{1,0:T(8,128)(2,1)}) %all-gather.7.cloned.1.call-update) | async-done | bytes 2359312 | tf_op jit(solution)/shard_map/all_gather | solution.py:382
  367.6 10.4 %fusion.11 = (f32[512,1536]{1,0:T(8,128)}, f32[512,1536]{1,0:T(8,128)}) fusion(f32[1536]{0:T(1024)S(1)} %copy-done.221, bf16[512,768]{1,0:T(8,128)(2,1)S(1)} %all_gather.59, bf16[768,1536]{1,0:T(8,128)(2,1)} %all-gather.7.cloned.1.call-done), kind=kOutput, calls=%fused_computation.39 | convolution fusion | flops 1257504768 | bytes 9443328 | tf_op jit(solution)/shard_map/dot_general | solution.py:246
  378.0 52.7 %all-gather.9.cloned.1.call-done = bf16[1536,768]{0,1:T(8,128)(2,1)} async-done(((bf16[1536,48]{0,1:T(8,128)(2,1)}), bf16[1536,768]{0,1:T(8,128)(2,1)}) %all-gather.9.cloned.1.call-update) | async-done | bytes 2359312 | tf_op jit(solution)/shard_map/all_gather | solution.py:383
  430.7 6.1 fusion.35
  439.2 9.7 %fusion.10 = (f32[512,1536]{1,0:T(8,128)S(1)}, f32[512,1536]{1,0:T(8,128)S(1)}) fusion(f32[1536]{0:T(1024)} %param.28, bf16[512,768]{1,0:T(8,128)(2,1)S(1)} %all_gather.57, bf16[768,1536]{1,0:T(8,128)(2,1)} %all-gather.7.cloned.1.call-done), kind=kOutput, calls=%fused_computation.38 | convolution fusion | flops 1257504768 | bytes 9443328 | tf_op jit(solution)/shard_map/dot_general | solution.py:246
  456.7 9.5 %fusion.9 = (f32[512,1536]{1,0:T(8,128)S(1)}, f32[512,1536]{1,0:T(8,128)S(1)}) fusion(f32[1536]{0:T(1024)} %param.28, bf16[512,768]{1,0:T(8,128)(2,1)S(1)} %all_gather.55, bf16[768,1536]{1,0:T(8,128)(2,1)} %all-gather.7.cloned.1.call-done), kind=kOutput, calls=%fused_computation.37 | convolution fusion | flops 1257504768 | bytes 9443328 | tf_op jit(solution)/shard_map/dot_general | solution.py:246
  473.5 5.7 reduce-scatter.23.cloned.1.call-done
  486.1 8.1 fusion.8
  499.5 10.4 %reduce-scatter.19.cloned.1.call-done = f32[256,768]{1,0:T(8,128)} async-done(((f32[512,768]{1,0:T(8,128)}), f32[256,768]{1,0:T(8,128)}) %reduce-scatter.19.cloned.1.call-update) | async-done | bytes 786448 | tf_op jit(solution)/shard_map/reduce_scatter | solution.py:256
  519.9 7.8 fusion.43
  537.8 7.8 fusion.42
  549.6 8.1 fusion.40
  561.6 7.8 fusion.41
  569.5 46.8 %all_gather.62 = bf16[384,768]{0,1:T(8,128)(2,1)} all-gather(bf16[384,48]{0,1:T(8,128)(2,1)} %param.26), channel_id=1, replica_groups=mesh['dp'=16,'tensor'=2] {'dp'}, dimensions={1}, use_global_device_ids=true | all-gather | bytes 626688 | tf_op jit(solution)/shard_map/all_gather | solution.py:393
  658.9 4.8 multiply_reduce_fusion.3
  671.7 4.8 multiply_reduce_fusion.2
  681.4 5.3 multiply_reduce_fusion
  690.3 7.1 multiply_convert_fusion.2
  699.2 4.9 multiply_convert_fusion.1
  745.0 71.8 %psum.34 = f32[2,8,384]{2,1,0:T(8,128)} all-reduce(f32[2,8,384]{2,1,0:T(8,128)S(1)} %fusion.110), channel_id=1, replica_groups=mesh['dp'=16,'tensor'=2] {'dp'}, use_global_device_ids=true, to_apply=%region_60.61 | all-reduce | flops 6144 | bytes 49152 | tf_op jit(solution)/shard_map/psum | solution.py:405
  (773 shorter events, 274.6 us)
Async XLA Ops:
  8.0 300.9 %reduce-scatter.21.cloned.1.call-start = ((), (), s32[]{:S(2)}) async-start(), calls=%async_computation.20 | async-start | bytes 2359296 | tf_op jit(solution)/shard_map/reduce_scatter | solution.py:237
  8.0 200.7 %collective-permute-start = (bf16[384,48]{0,1:T(8,128)(2,1)}, bf16[384,48]{0,1:T(8,128)(2,1)}, u32[]{:S(2)}, u32[]{:S(2)}) collective-permute-start(bf16[384,48]{0,1:T(8,128)(2,1)} %param.26), channel_id=1, source_target_pairs={{0,2},{2,4},{4,6},{6,8},{8,10},{10,12},{12,14},{14,16},{16,18},{18... | collective-permute-start | bytes 110600 | tf_op jit(solution)/shard_map/ppermute | solution.py:24
  11.1 199.3 %collective-permute-start.1 = (bf16[384,48]{0,1:T(8,128)(2,1)}, bf16[384,48]{0,1:T(8,128)(2,1)}, u32[]{:S(2)}, u32[]{:S(2)}) collective-permute-start(bf16[384,48]{0,1:T(8,128)(2,1)} %param.26), channel_id=1, source_target_pairs={{0,30},{2,0},{4,2},{6,4},{8,6},{10,8},{12,10},{14,12},{16,14},{18,... | collective-permute-start | bytes 110600 | tf_op jit(solution)/shard_map/ppermute | solution.py:30
  208.8 7.8 collective-permute-start.2
  216.6 7.6 collective-permute-start.4
  216.6 7.6 collective-permute-start.5
  224.2 7.6 collective-permute-start.6
  224.2 7.6 collective-permute-start.7
  231.7 7.6 collective-permute-start.8
  231.7 7.6 collective-permute-start.9
  239.3 7.6 collective-permute-start.10
  239.3 7.6 collective-permute-start.11
  246.8 7.6 collective-permute-start.12
  246.8 7.6 collective-permute-start.13
  254.4 7.6 collective-permute-start.14
  265.9 43.0 %reduce-scatter.17.cloned.1.call-start = ((), (), s32[]{:S(2)}) async-start(), calls=%async_computation.16 | async-start | bytes 2359296 | tf_op jit(solution)/shard_map/reduce_scatter | solution.py:237
  282.1 26.8 %reduce-scatter.29.cloned.1.call-start = ((), (), s32[]{:S(2)}) async-start(), calls=%async_computation.24 | async-start | bytes 2359296 | tf_op jit(solution)/shard_map/reduce_scatter | solution.py:237
  295.9 18.1 %reduce-scatter.25.cloned.1.call-start = ((), (), s32[]{:S(2)}) async-start(), calls=%async_computation.22 | async-start | bytes 2359296 | tf_op jit(solution)/shard_map/reduce_scatter | solution.py:237
  306.4 61.2 %all-gather.7.cloned.1.call-start = ((), (), s32[]{:S(2)}) async-start(), calls=%async_computation.17 | async-start | bytes 2506752 | tf_op jit(solution)/shard_map/all_gather | solution.py:382
  307.0 123.7 %all-gather.9.cloned.1.call-start = ((), (), s32[]{:S(2)}) async-start(), calls=%async_computation.18 | async-start | bytes 2506752 | tf_op jit(solution)/shard_map/all_gather | solution.py:383
  307.5 165.9 %reduce-scatter.31.cloned.1.call-start = ((), (), s32[]{:S(2)}) async-start(), calls=%async_computation.25 | async-start | bytes 2359296 | tf_op jit(solution)/shard_map/reduce_scatter | solution.py:256
  436.8 36.7 %reduce-scatter.27.cloned.1.call-start = ((), (), s32[]{:S(2)}) async-start(), calls=%async_computation.23 | async-start | bytes 2359296 | tf_op jit(solution)/shard_map/reduce_scatter | solution.py:256
  454.3 24.9 %reduce-scatter.23.cloned.1.call-start = ((), (), s32[]{:S(2)}) async-start(), calls=%async_computation.21 | async-start | bytes 2359296 | tf_op jit(solution)/shard_map/reduce_scatter | solution.py:256
  471.6 38.3 %reduce-scatter.19.cloned.1.call-start = ((), (), s32[]{:S(2)}) async-start(), calls=%async_computation.19 | async-start | bytes 2359296 | tf_op jit(solution)/shard_map/reduce_scatter | solution.py:256
  499.4 119.6 %reduce-scatter.45.cloned.1.call-start = ((), (), s32[]{:S(2)}) async-start(), calls=%async_computation.32 | async-start | bytes 2359296 | tf_op jit(solution)/shard_map/reduce_scatter | solution.py:298
  527.8 91.2 %reduce-scatter.41.cloned.1.call-start = ((), (), s32[]{:S(2)}) async-start(), calls=%async_computation.30 | async-start | bytes 2359296 | tf_op jit(solution)/shard_map/reduce_scatter | solution.py:298
  545.6 73.4 %reduce-scatter.33.cloned.1.call-start = ((), (), s32[]{:S(2)}) async-start(), calls=%async_computation.26 | async-start | bytes 2359296 | tf_op jit(solution)/shard_map/reduce_scatter | solution.py:298
  557.8 64.5 %reduce-scatter.37.cloned.1.call-start = ((), (), s32[]{:S(2)}) async-start(), calls=%async_computation.28 | async-start | bytes 2359296 | tf_op jit(solution)/shard_map/reduce_scatter | solution.py:298
  569.5 247.3 %reduce-scatter.35.cloned.1.call-start = ((), (), s32[]{:S(2)}) async-start(), calls=%async_computation.27 | async-start | bytes 1179648 | tf_op jit(solution)/shard_map/reduce_scatter | solution.py:326
  690.2 128.6 %reduce-scatter.39.cloned.1.call-start = ((), (), s32[]{:S(2)}) async-start(), calls=%async_computation.29 | async-start | bytes 1179648 | tf_op jit(solution)/shard_map/reduce_scatter | solution.py:326
  718.5 102.4 %reduce-scatter.43.cloned.1.call-start = ((), (), s32[]{:S(2)}) async-start(), calls=%async_computation.31 | async-start | bytes 1179648 | tf_op jit(solution)/shard_map/reduce_scatter | solution.py:326
  728.3 94.7 %reduce-scatter.47.cloned.1.call-start = ((), (), s32[]{:S(2)}) async-start(), calls=%async_computation.33 | async-start | bytes 1179648 | tf_op jit(solution)/shard_map/reduce_scatter | solution.py:326
  (242 other events, 2996.1 us)
Sparse Core Ops, SparseCore 0:
  266.0 4.9 reduce-scatter.20
  282.2 4.9 reduce-scatter.16
  296.0 4.9 reduce-scatter.28
  306.5 7.4 reduce-scatter.24
  436.9 7.4 reduce-scatter.30
  454.4 7.4 reduce-scatter.26
  471.7 7.4 reduce-scatter.22
  499.5 10.3 reduce-scatter.18
  527.9 10.3 reduce-scatter.44
  545.7 10.3 reduce-scatter.40
  558.9 10.3 reduce-scatter.32
  571.4 10.3 reduce-scatter.36
  690.3 4.0 reduce-scatter.34
  718.6 4.0 reduce-scatter.38
  728.4 5.6 reduce-scatter.42
  737.8 8.2 reduce-scatter.46
Sparse Core Ops, SparseCore 1:
  309.7 57.8 all-gather.6
  370.2 60.4 all-gather.8
